TPU v7x, 32 devices: a whole 2x2x4 slice. The times are simulated.
32 devices in a mesh: tok: 8 (over z, y), vocab: 4 (over x, core).
Axes of the slice: x: 2, y: 2, z: 4, core: 2. Of those that a mesh axis runs over, the one named last changes fastest.
Arguments:
- hidden: bfloat16 [192, 9216], P('tok'), may hold values from -256 to 256
- policy_head: bfloat16 [9216, 32768], P(None, ('tok', 'vocab')), may hold values from -0.0625 to 0.0625
- reference_head: bfloat16 [9216, 32768], P(None, ('tok', 'vocab')), may hold values from -0.0625 to 0.0625
- targets: int32 [192], P('tok'), may hold values from 0 to 32767
Outputs:
- policy_logprob: float32 [192], P('tok')
- reference_logprob: float32 [192], P('tok')
- divergence: float32 [192], P('tok')
All inputs are finite; a program needn't handle non-finite values.
Results may differ from a plain program's by a relative error of at most 0.00055.
Values may be sent and summed in bfloat16 or wider, within the bound.
A program may use at most 128 MiB of HBM per device.

v0:
```python
import jax
import jax.numpy as jnp
from jax import lax
from jax.sharding import PartitionSpec as P


def combined_all(value, axis, combine):
    everything = jax.tree.map(lambda part: lax.all_gather(part, axis), value)
    leading = jax.tree.map(lambda part: part[0], everything)

    def step(k, so_far):
        return combine(so_far, jax.tree.map(lambda part: part[k], everything))

    return lax.fori_loop(1, lax.axis_size(axis), step, leading)


def local_sums(policy_logits, reference_logits, target_hits, peak_policy, peak_reference):
    policy_exp = jnp.exp(policy_logits - peak_policy[:, None])
    reference_exp = jnp.exp(reference_logits - peak_reference[:, None])
    total_policy = jnp.sum(policy_exp, axis=1)
    total_reference = jnp.sum(reference_exp, axis=1)
    weighted = jnp.sum(policy_exp * (policy_logits - reference_logits), axis=1)
    target_policy = jnp.sum(jnp.where(target_hits, policy_logits, 0.0), axis=1)
    target_reference = jnp.sum(jnp.where(target_hits, reference_logits, 0.0), axis=1)
    return (total_policy, total_reference, weighted, target_policy, target_reference)


def local_stats(policy_logits, reference_logits, target_hits):
    peak_policy = jnp.max(policy_logits, axis=1)
    peak_reference = jnp.max(reference_logits, axis=1)
    summed = local_sums(policy_logits, reference_logits, target_hits, peak_policy, peak_reference)
    return (peak_policy, peak_reference) + summed


def combine_stats(left_stats, right_stats):
    peak_policy = jnp.maximum(left_stats[0], right_stats[0])
    peak_reference = jnp.maximum(left_stats[1], right_stats[1])
    left_policy = jnp.exp(left_stats[0] - peak_policy)
    right_policy = jnp.exp(right_stats[0] - peak_policy)
    left_reference = jnp.exp(left_stats[1] - peak_reference)
    right_reference = jnp.exp(right_stats[1] - peak_reference)
    return (
        peak_policy,
        peak_reference,
        left_stats[2] * left_policy + right_stats[2] * right_policy,
        left_stats[3] * left_reference + right_stats[3] * right_reference,
        left_stats[4] * left_policy + right_stats[4] * right_policy,
        left_stats[5] + right_stats[5],
        left_stats[6] + right_stats[6],
    )


def combine_senders(received):
    peak_policy = jnp.max(received[0], axis=0)
    peak_reference = jnp.max(received[1], axis=0)
    policy_scale = jnp.exp(received[0] - peak_policy[None, :])
    reference_scale = jnp.exp(received[1] - peak_reference[None, :])
    return (
        peak_policy,
        peak_reference,
        jnp.sum(received[2] * policy_scale, axis=0),
        jnp.sum(received[3] * reference_scale, axis=0),
        jnp.sum(received[4] * policy_scale, axis=0),
        jnp.sum(received[5], axis=0),
        jnp.sum(received[6], axis=0),
    )


def finish(merged_stats):
    log_norm_policy = merged_stats[0] + jnp.log(merged_stats[2])
    log_norm_reference = merged_stats[1] + jnp.log(merged_stats[3])
    policy_logprob = merged_stats[5] - log_norm_policy
    reference_logprob = merged_stats[6] - log_norm_reference
    divergence = merged_stats[4] / merged_stats[2] - log_norm_policy + log_norm_reference
    return (policy_logprob, reference_logprob, divergence)


def body(hidden, policy_head, reference_head, targets):
    tok_count = lax.axis_size("tok")
    vocab_count = lax.axis_size("vocab")
    tok_rows = hidden.shape[0]
    vocab_cols = policy_head.shape[1]
    piece = lax.all_gather(hidden, "tok", axis=0, tiled=True)
    summed = jnp.concatenate(
        [
            jnp.dot(piece, policy_head, preferred_element_type=jnp.float32),
            jnp.dot(piece, reference_head, preferred_element_type=jnp.float32),
        ],
        axis=1,
    )
    policy_logits = summed[:, :vocab_cols]
    reference_logits = summed[:, vocab_cols:]
    every_target = lax.all_gather(targets, "tok", axis=0, tiled=True)
    block_index = lax.axis_index("tok") * vocab_count + lax.axis_index("vocab")
    vocab_ids = block_index * vocab_cols + lax.iota(jnp.int32, vocab_cols)
    target_hits = vocab_ids[None, :] == every_target[:, None]
    partial_value = local_stats(policy_logits, reference_logits, target_hits)
    shaped = tuple((entry.reshape(tok_count, tok_rows) for entry in partial_value))
    received = lax.all_to_all(shaped, "tok", split_axis=0, concat_axis=0, tiled=True)
    own_stats = combine_senders(received)
    merged_stats = combined_all(own_stats, "vocab", combine_stats)
    return finish(merged_stats)


def solution(mesh):
    in_specs = (P("tok", None), P(None, ("tok", "vocab")), P(None, ("tok", "vocab")), P("tok"))
    out_specs = (P("tok"), P("tok"), P("tok"))
    return jax.shard_map(body, mesh=mesh, in_specs=in_specs, out_specs=out_specs, check_vma=False)
```

profile of v0, /device:TPU:0, one launch (start us, length us, event | category | flops | bytes accessed | tf_op | source)
XLA Modules:
  0.0 179.8 jit_solution(15287167651976823062)
XLA Ops:
  7.2 0.7 all-gather.9.cloned.1.call-update
  7.9 1.2 dynamic-slice.5
  9.8 0.9 dynamic-update-slice.5
  10.7 13.1 %all-reduce.5 = s32[192]{0:T(256)S(1)} all-reduce(s32[192]{0:T(256)S(1)} %dynamic-update-slice.5), channel_id=1, replica_groups=mesh['tok'=8,'vocab'=4] {'tok'}, use_global_device_ids=true, to_apply=%add.5 | all-reduce | flops 192 | bytes 1536
  23.8 53.8 %all-gather.9.cloned.1.call-done = bf16[192,9216]{1,0:T(8,128)(2,1)} async-done(((bf16[24,9216]{1,0:T(8,128)(2,1)}), bf16[192,9216]{1,0:T(8,128)(2,1)}) %all-gather.9.cloned.1.call-update) | async-done | bytes 3538960 | tf_op jit(solution)/shard_map/all_gather | solution.py:83
  77.5 9.6 %fusion.24 = (f32[192]{0:T(256)S(1)}, f32[192,1024]{1,0:T(8,128)S(1)}) fusion(bf16[192,9216]{1,0:T(8,128)(2,1)} %all-gather.9.cloned.1.call-done, bf16[9216,1024]{1,0:T(8,128)(2,1)} %param.7), kind=kOutput, calls=%fused_computation.44 | convolution fusion | flops 3624075008 | bytes 23200512 | tf_op jit(solution)/shard_map/dot_general | solution.py:86
  87.2 3.1 %copy-done = bf16[9216,1024]{1,0:T(8,128)(2,1)S(1)} copy-done((bf16[9216,1024]{1,0:T(8,128)(2,1)S(1)}, bf16[9216,1024]{1,0:T(8,128)(2,1)}, u32[]{:S(2)}) %copy-start) | copy-done | bytes 18874392
  90.3 5.9 %fusion.25 = (f32[192]{0:T(256)S(1)}, f32[192,1024]{1,0:T(8,128)S(1)}) fusion(bf16[192,9216]{1,0:T(8,128)(2,1)} %all-gather.9.cloned.1.call-done, bf16[9216,1024]{1,0:T(8,128)(2,1)S(1)} %copy-done), kind=kOutput, calls=%fused_computation.45 | convolution fusion | flops 3624075008 | bytes 23200512 | tf_op jit(solution)/shard_map/dot_general | solution.py:87
  96.2 0.7 multiply_reduce_fusion
  96.9 0.7 all_to_all.64
  97.5 3.3 %all-to-all-start.4 = ((f32[8,1,24]{2,1,0:T(1,128)}), f32[8,1,24]{2,1,0:T(1,128)S(1)}, u32[]{:S(2)}, u32[]{:S(2)}) async-start(f32[8,1,24]{2,1,0:T(1,128)} %all_to_all.64), calls=%async_computation.4 | async-start | bytes 8192 | tf_op jit(solution)/shard_map/all_to_all | solution.py:99
  100.9 0.7 all_to_all.56
  101.6 5.8 %all-to-all-done.4 = f32[8,1,24]{2,1,0:T(1,128)S(1)} async-done(((f32[8,1,24]{2,1,0:T(1,128)}), f32[8,1,24]{2,1,0:T(1,128)S(1)}, u32[]{:S(2)}, u32[]{:S(2)}) %all-to-all-start.4) | async-done | bytes 800 | tf_op jit(solution)/shard_map/all_to_all | solution.py:99
  107.4 3.2 %all-to-all-start.2 = ((f32[8,1,24]{2,1,0:T(1,128)}), f32[8,1,24]{2,1,0:T(1,128)S(1)}, u32[]{:S(2)}, u32[]{:S(2)}) async-start(f32[8,1,24]{2,1,0:T(1,128)} %all_to_all.56), calls=%async_computation.2 | async-start | bytes 8192 | tf_op jit(solution)/shard_map/all_to_all | solution.py:99
  110.6 0.7 all_to_all.52
  111.3 5.7 %all-to-all-done.2 = f32[8,1,24]{2,1,0:T(1,128)S(1)} async-done(((f32[8,1,24]{2,1,0:T(1,128)}), f32[8,1,24]{2,1,0:T(1,128)S(1)}, u32[]{:S(2)}, u32[]{:S(2)}) %all-to-all-start.2) | async-done | bytes 800 | tf_op jit(solution)/shard_map/all_to_all | solution.py:99
  117.1 3.3 %all-to-all-start = ((f32[8,1,24]{2,1,0:T(1,128)}), f32[8,1,24]{2,1,0:T(1,128)S(1)}, u32[]{:S(2)}, u32[]{:S(2)}) async-start(f32[8,1,24]{2,1,0:T(1,128)} %all_to_all.52), calls=%async_computation | async-start | bytes 8192 | tf_op jit(solution)/shard_map/all_to_all | solution.py:99
  120.4 0.7 all_to_all.60
  121.1 5.8 %all-to-all-done = f32[8,1,24]{2,1,0:T(1,128)S(1)} async-done(((f32[8,1,24]{2,1,0:T(1,128)}), f32[8,1,24]{2,1,0:T(1,128)S(1)}, u32[]{:S(2)}, u32[]{:S(2)}) %all-to-all-start) | async-done | bytes 800 | tf_op jit(solution)/shard_map/all_to_all | solution.py:99
  126.8 3.2 %all-to-all-start.3 = ((f32[8,1,24]{2,1,0:T(1,128)}), f32[8,1,24]{2,1,0:T(1,128)S(1)}, u32[]{:S(2)}, u32[]{:S(2)}) async-start(f32[8,1,24]{2,1,0:T(1,128)} %all_to_all.60), calls=%async_computation.3 | async-start | bytes 8192 | tf_op jit(solution)/shard_map/all_to_all | solution.py:99
  130.1 0.7 all_to_all.54
  130.8 5.7 %all-to-all-done.3 = f32[8,1,24]{2,1,0:T(1,128)S(1)} async-done(((f32[8,1,24]{2,1,0:T(1,128)}), f32[8,1,24]{2,1,0:T(1,128)S(1)}, u32[]{:S(2)}, u32[]{:S(2)}) %all-to-all-start.3) | async-done | bytes 800 | tf_op jit(solution)/shard_map/all_to_all | solution.py:99
  136.5 3.3 %all-to-all-start.1 = ((f32[8,1,24]{2,1,0:T(1,128)}), f32[8,1,24]{2,1,0:T(1,128)S(1)}, u32[]{:S(2)}, u32[]{:S(2)}) async-start(f32[8,1,24]{2,1,0:T(1,128)} %all_to_all.54), calls=%async_computation.1 | async-start | bytes 8192 | tf_op jit(solution)/shard_map/all_to_all | solution.py:99
  139.9 0.6 dynamic-slice
  141.1 0.7 all_to_all.67
  141.8 0.7 all_to_all.69
  142.5 3.8 %all-to-all-done.1 = f32[8,1,24]{2,1,0:T(1,128)S(1)} async-done(((f32[8,1,24]{2,1,0:T(1,128)}), f32[8,1,24]{2,1,0:T(1,128)S(1)}, u32[]{:S(2)}, u32[]{:S(2)}) %all-to-all-start.1) | async-done | bytes 800 | tf_op jit(solution)/shard_map/all_to_all | solution.py:99
  146.3 3.2 %all-to-all-start.5 = ((f32[8,1,24]{2,1,0:T(1,128)}), f32[8,1,24]{2,1,0:T(1,128)S(1)}, u32[]{:S(2)}, u32[]{:S(2)}) async-start(f32[8,1,24]{2,1,0:T(1,128)} %all_to_all.67), calls=%async_computation.5 | async-start | bytes 8192 | tf_op jit(solution)/shard_map/all_to_all | solution.py:99
  149.6 6.4 %all-to-all-done.5 = f32[8,1,24]{2,1,0:T(1,128)S(1)} async-done(((f32[8,1,24]{2,1,0:T(1,128)}), f32[8,1,24]{2,1,0:T(1,128)S(1)}, u32[]{:S(2)}, u32[]{:S(2)}) %all-to-all-start.5) | async-done | bytes 800 | tf_op jit(solution)/shard_map/all_to_all | solution.py:99
  156.0 3.3 %all-to-all-start.6 = ((f32[8,1,24]{2,1,0:T(1,128)}), f32[8,1,24]{2,1,0:T(1,128)S(1)}, u32[]{:S(2)}, u32[]{:S(2)}) async-start(f32[8,1,24]{2,1,0:T(1,128)} %all_to_all.69), calls=%async_computation.6 | async-start | bytes 8192 | tf_op jit(solution)/shard_map/all_to_all | solution.py:99
  159.3 0.2 dynamic-update-slice
  159.5 0.2 dynamic-update-slice.1
  159.7 0.2 dynamic-update-slice.4
  159.9 0.2 dynamic-update-slice.2
  160.1 0.2 dynamic-update-slice.3
  160.4 0.2 dynamic-update-slice.6
  160.6 5.1 %all-to-all-done.6 = f32[8,1,24]{2,1,0:T(1,128)S(1)} async-done(((f32[8,1,24]{2,1,0:T(1,128)}), f32[8,1,24]{2,1,0:T(1,128)S(1)}, u32[]{:S(2)}, u32[]{:S(2)}) %all-to-all-start.6) | async-done | bytes 800 | tf_op jit(solution)/shard_map/all_to_all | solution.py:99
  165.7 0.2 dynamic-update-slice.7
  165.9 5.6 %all-reduce.8 = (f32[96]{0:T(128)S(1)}, f32[96]{0:T(128)S(1)}, f32[96]{0:T(128)S(1)}, f32[96]{0:T(128)S(1)}, f32[96]{0:T(128)S(1)}, /*index=5*/f32[96]{0:T(128)S(1)}, f32[96]{0:T(128)S(1)}) all-reduce(f32[96]{0:T(128)S(1)} %dynamic-update-slice, f32[96]{0:T(128)S(1)} %dynamic-update-slice.1, ...), channel_id=2, replica_groups=mesh['tok'=8,'vocab'=4] {'vocab'}, use_global_device_ids=true, to_apply=%add | all-reduce | flops 672 | bytes 5376
  171.6 0.1 reshape.43
  171.7 0.1 reshape.44
  171.7 0.1 reshape.45
  171.8 0.1 reshape.46
  171.9 0.1 reshape.47
  172.0 0.1 reshape.48
  172.1 0.1 reshape.49
  172.2 0.3 while.27
  172.5 0.5 subtract_add_fusion
  (31 shorter events, 0.4 us)
Async XLA Ops:
  7.2 70.3 %all-gather.9.cloned.1.call-start = ((), (), s32[]{:S(2)}) async-start(), calls=%async_computation.7 | async-start | bytes 3981312 | tf_op jit(solution)/shard_map/all_gather | solution.py:83
  77.5 12.7 %copy-start = (bf16[9216,1024]{1,0:T(8,128)(2,1)S(1)}, bf16[9216,1024]{1,0:T(8,128)(2,1)}, u32[]{:S(2)}) copy-start(bf16[9216,1024]{1,0:T(8,128)(2,1)} %param.8) | copy-start | bytes 56623108
  90.3 49.6 %copy-start.1 = (u32[32]{0:T(128)S(1)}, u32[32]{0:T(128)}, u32[]{:S(2)}) copy-start(u32[32]{0:T(128)} %constant.57) | copy-start | bytes 388
  97.5 9.8 %all-to-all-start.4 = ((f32[8,1,24]{2,1,0:T(1,128)}), f32[8,1,24]{2,1,0:T(1,128)S(1)}, u32[]{:S(2)}, u32[]{:S(2)}) async-start(f32[8,1,24]{2,1,0:T(1,128)} %all_to_all.64), calls=%async_computation.4 | async-start | bytes 8192 | tf_op jit(solution)/shard_map/all_to_all | solution.py:99
  107.4 9.7 %all-to-all-start.2 = ((f32[8,1,24]{2,1,0:T(1,128)}), f32[8,1,24]{2,1,0:T(1,128)S(1)}, u32[]{:S(2)}, u32[]{:S(2)}) async-start(f32[8,1,24]{2,1,0:T(1,128)} %all_to_all.56), calls=%async_computation.2 | async-start | bytes 8192 | tf_op jit(solution)/shard_map/all_to_all | solution.py:99
  117.1 9.8 %all-to-all-start = ((f32[8,1,24]{2,1,0:T(1,128)}), f32[8,1,24]{2,1,0:T(1,128)S(1)}, u32[]{:S(2)}, u32[]{:S(2)}) async-start(f32[8,1,24]{2,1,0:T(1,128)} %all_to_all.52), calls=%async_computation | async-start | bytes 8192 | tf_op jit(solution)/shard_map/all_to_all | solution.py:99
  126.8 9.7 %all-to-all-start.3 = ((f32[8,1,24]{2,1,0:T(1,128)}), f32[8,1,24]{2,1,0:T(1,128)S(1)}, u32[]{:S(2)}, u32[]{:S(2)}) async-start(f32[8,1,24]{2,1,0:T(1,128)} %all_to_all.60), calls=%async_computation.3 | async-start | bytes 8192 | tf_op jit(solution)/shard_map/all_to_all | solution.py:99
  136.5 9.8 %all-to-all-start.1 = ((f32[8,1,24]{2,1,0:T(1,128)}), f32[8,1,24]{2,1,0:T(1,128)S(1)}, u32[]{:S(2)}, u32[]{:S(2)}) async-start(f32[8,1,24]{2,1,0:T(1,128)} %all_to_all.54), calls=%async_computation.1 | async-start | bytes 8192 | tf_op jit(solution)/shard_map/all_to_all | solution.py:99
  146.3 9.7 %all-to-all-start.5 = ((f32[8,1,24]{2,1,0:T(1,128)}), f32[8,1,24]{2,1,0:T(1,128)S(1)}, u32[]{:S(2)}, u32[]{:S(2)}) async-start(f32[8,1,24]{2,1,0:T(1,128)} %all_to_all.67), calls=%async_computation.5 | async-start | bytes 8192 | tf_op jit(solution)/shard_map/all_to_all | solution.py:99
  156.0 9.7 %all-to-all-start.6 = ((f32[8,1,24]{2,1,0:T(1,128)}), f32[8,1,24]{2,1,0:T(1,128)S(1)}, u32[]{:S(2)}, u32[]{:S(2)}) async-start(f32[8,1,24]{2,1,0:T(1,128)} %all_to_all.69), calls=%async_computation.6 | async-start | bytes 8192 | tf_op jit(solution)/shard_map/all_to_all | solution.py:99
Sparse Core Ops, SparseCore 0:
  10.2 67.3 all-gather.8
where the time goes:
time: 180 us
  waiting for transfers between devices  92.7 us (52%)
  starting transfers between devices  23.1 us (13%)
  blocking collectives  18.7 us (10%)
  matrix products  15.6 us (9%)
  between operations  15.5 us (9%)
  local copies, waits for them, and re-layouts  12.7 us (7%)
    all_gather x1, waiting for transfers between devices, body(): piece = lax.all_gather(hidden, 'tok', axis=0, tiled=True)  53.8 us
    all_to_all x7, waiting for transfers between devices, body(): lax.all_to_all(shaped, 'tok', split_axis=0, concat_axis=0, tiled=True)  38.3 us
    all_to_all x7, starting transfers between devices, body(): lax.all_to_all(shaped, 'tok', split_axis=0, concat_axis=0, tiled=True)  23 us
    unnamed x2, blocking collectives  18.7 us
    dot_general x1, matrix products, body(): jnp.dot(piece, policy_head, preferred_element_type=jnp.float32)  9.63 us
    unnamed x22, local copies, waits for them, and re-layouts  7.34 us
    dot_general x1, matrix products, body(): jnp.dot(piece, reference_head, preferred_element_type=jnp.float32)  5.92 us
    all_to_all x7, local copies, waits for them, and re-layouts, body(): lax.all_to_all(shaped, 'tok', split_axis=0, concat_axis=0, tiled=True)  4.75 us
  transfers between devices with their start and end apart: 8, of which 8 were waited for; matrix products, arithmetic and copies ran while one was open for 2% of the time, Pallas kernels for 0%

commit v1 on v0

--- a/solution.py
+++ b/solution.py
@@ -80,7 +80,14 @@
     vocab_count = lax.axis_size("vocab")
     tok_rows = hidden.shape[0]
     vocab_cols = policy_head.shape[1]
-    piece = lax.all_gather(hidden, "tok", axis=0, tiled=True)
+    ways = lax.axis_size("tok")
+    pieces = [hidden]
+    for far in range(1, ways):
+        pieces.append(
+            lax.ppermute(pieces[far - 1], "tok", [(d, (d - 1) % ways) for d in range(ways)])
+        )
+    line = jnp.concatenate(pieces, axis=0)
+    piece = jnp.roll(line, lax.axis_index("tok") * hidden.shape[0], axis=0)
     summed = jnp.concatenate(
         [
             jnp.dot(piece, policy_head, preferred_element_type=jnp.float32),

time: 180 us -> 195 us (1.083)
  starting transfers between devices: 23.1 us -> 57.8 us
  waiting for transfers between devices: 92.7 us -> 75.2 us
  between operations: 15.5 us -> 2.09 us
  local copies, waits for them, and re-layouts: 12.7 us -> 23.4 us
  matrix products: 15.6 us -> 18.2 us
  blocking collectives: 18.7 us -> 16.1 us
    all_gather x1 -> x0, waiting for transfers between devices: 53.8 us -> none  [body(): piece = lax.all_gather(hidden, 'tok', axis=0, tiled=True)]
    ppermute x0 -> x7, waiting for transfers between devices: none -> 36.9 us  [body(): lax.ppermute(pieces[far - 1], 'tok', [(d, (d - 1) % ways) for d in range(...]
    ppermute x0 -> x7, starting transfers between devices: none -> 31.6 us  [body(): lax.ppermute(pieces[far - 1], 'tok', [(d, (d - 1) % ways) for d in range(...]
    unnamed x22 -> x39, local copies, waits for them, and re-layouts: 7.34 us -> 17.3 us
    dot_general x1, matrix products: 5.92 us -> 9.63 us  [body(): jnp.dot(piece, reference_head, preferred_element_type=jnp.float32)]
    all_to_all x7, starting transfers between devices: 23 us -> 26.2 us  [body(): lax.all_to_all(shaped, 'tok', split_axis=0, concat_axis=0, tiled=True)]
    unnamed x2, blocking collectives: 18.7 us -> 16.1 us
  transfers between devices with their start and end apart: 8 -> 14, of which waited for: 8 -> 13; matrix products, arithmetic and copies ran while one was open for 2% -> 6% of each run, Pallas kernels for 0% -> 0%
where the time goes in v1:
time: 195 us
  waiting for transfers between devices  75.2 us (39%)
  starting transfers between devices  57.8 us (30%)
  local copies, waits for them, and re-layouts  23.4 us (12%)
  matrix products  18.2 us (9%)
  blocking collectives  16.1 us (8%)
  between operations  2.09 us (1%)
    all_to_all x7, waiting for transfers between devices, body(): lax.all_to_all(shaped, 'tok', split_axis=0, concat_axis=0, tiled=True)  38.3 us
    ppermute x7, waiting for transfers between devices, body(): lax.ppermute(pieces[far - 1], 'tok', [(d, (d - 1) % ways) for d in range(...  36.9 us
    ppermute x7, starting transfers between devices, body(): lax.ppermute(pieces[far - 1], 'tok', [(d, (d - 1) % ways) for d in range(...  31.6 us
    all_to_all x7, starting transfers between devices, body(): lax.all_to_all(shaped, 'tok', split_axis=0, concat_axis=0, tiled=True)  26.2 us
    unnamed x39, local copies, waits for them, and re-layouts  17.3 us
    unnamed x2, blocking collectives  16.1 us
    dot_general x1, matrix products, body(): jnp.dot(piece, reference_head, preferred_element_type=jnp.float32)  9.63 us
    dot_general x1, matrix products, body(): jnp.dot(piece, policy_head, preferred_element_type=jnp.float32)  8.61 us
  transfers between devices with their start and end apart: 14, of which 13 were waited for; matrix products, arithmetic and copies ran while one was open for 6% of the time, Pallas kernels for 0%

profile of v1, /device:TPU:0, one launch (start us, length us, event | category | flops | bytes accessed | tf_op | source)
XLA Modules:
  0.0 194.6 jit_solution(13074831542316297697)
XLA Ops:
  0.6 6.1 %collective-permute-start = (bf16[24,9216]{1,0:T(8,128)(2,1)}, bf16[24,9216]{1,0:T(8,128)(2,1)S(1)}, u32[]{:S(2)}, u32[]{:S(2)}) collective-permute-start(bf16[24,9216]{1,0:T(8,128)(2,1)} %param.6), channel_id=1, source_target_pairs={{0,28},{4,0},{8,4},{12,8},{16,12},{20,16},{24,20},{28,24},{1,29},{... | collective-permute-start | bytes 1327112 | tf_op jit(solution)/shard_map/ppermute | solution.py:87
  6.7 1.8 constant_dynamic-update-slice_fusion.15
  8.6 1.2 dynamic-slice.5
  10.5 0.9 dynamic-update-slice.5
  11.3 10.4 %all-reduce.5 = s32[192]{0:T(256)S(1)} all-reduce(s32[192]{0:T(256)S(1)} %dynamic-update-slice.5), channel_id=1, replica_groups=mesh['tok'=8,'vocab'=4] {'tok'}, use_global_device_ids=true, to_apply=%add.5 | all-reduce | flops 192 | bytes 1536
  21.8 1.2 collective-permute-start.1
  23.0 0.8 constant_dynamic-update-slice_fusion.14
  23.8 8.3 %collective-permute-done.1 = bf16[24,9216]{1,0:T(8,128)(2,1)S(1)} collective-permute-done((bf16[24,9216]{1,0:T(8,128)(2,1)S(1)}, bf16[24,9216]{1,0:T(8,128)(2,1)S(1)}, u32[]{:S(2)}, u32[]{:S(2)}) %collective-permute-start.1) | collective-permute-done | bytes 442400 | tf_op jit(solution)/shard_map/ppermute | solution.py:87
  32.1 3.6 %collective-permute-start.2 = (bf16[24,9216]{1,0:T(8,128)(2,1)S(1)}, bf16[24,9216]{1,0:T(8,128)(2,1)S(1)}, u32[]{:S(2)}, u32[]{:S(2)}) collective-permute-start(bf16[24,9216]{1,0:T(8,128)(2,1)S(1)} %collective-permute-done.1), channel_id=1, source_target_pairs={{0,28},{4,0},{8,4},{12,8},{16,12},{20,16},{24,20},{28,24},{1,29},{... | collective-permute-start | bytes 1327112 | tf_op jit(solution)/shard_map/ppermute | solution.py:87
  35.7 0.8 constant_dynamic-update-slice_fusion.13
  36.5 5.8 %collective-permute-done.2 = bf16[24,9216]{1,0:T(8,128)(2,1)S(1)} collective-permute-done((bf16[24,9216]{1,0:T(8,128)(2,1)S(1)}, bf16[24,9216]{1,0:T(8,128)(2,1)S(1)}, u32[]{:S(2)}, u32[]{:S(2)}) %collective-permute-start.2) | collective-permute-done | bytes 442400 | tf_op jit(solution)/shard_map/ppermute | solution.py:87
  42.3 5.2 %collective-permute-start.3 = (bf16[24,9216]{1,0:T(8,128)(2,1)S(1)}, bf16[24,9216]{1,0:T(8,128)(2,1)S(1)}, u32[]{:S(2)}, u32[]{:S(2)}) collective-permute-start(bf16[24,9216]{1,0:T(8,128)(2,1)S(1)} %collective-permute-done.2), channel_id=1, source_target_pairs={{0,28},{4,0},{8,4},{12,8},{16,12},{20,16},{24,20},{28,24},{1,29},{... | collective-permute-start | bytes 1327112 | tf_op jit(solution)/shard_map/ppermute | solution.py:87
  47.5 0.8 constant_dynamic-update-slice_fusion.12
  48.3 5.0 %collective-permute-done.3 = bf16[24,9216]{1,0:T(8,128)(2,1)S(1)} collective-permute-done((bf16[24,9216]{1,0:T(8,128)(2,1)S(1)}, bf16[24,9216]{1,0:T(8,128)(2,1)S(1)}, u32[]{:S(2)}, u32[]{:S(2)}) %collective-permute-start.3) | collective-permute-done | bytes 442400 | tf_op jit(solution)/shard_map/ppermute | solution.py:87
  53.3 5.2 %collective-permute-start.4 = (bf16[24,9216]{1,0:T(8,128)(2,1)S(1)}, bf16[24,9216]{1,0:T(8,128)(2,1)S(1)}, u32[]{:S(2)}, u32[]{:S(2)}) collective-permute-start(bf16[24,9216]{1,0:T(8,128)(2,1)S(1)} %collective-permute-done.3), channel_id=1, source_target_pairs={{0,28},{4,0},{8,4},{12,8},{16,12},{20,16},{24,20},{28,24},{1,29},{... | collective-permute-start | bytes 1327112 | tf_op jit(solution)/shard_map/ppermute | solution.py:87
  58.5 0.8 constant_dynamic-update-slice_fusion.11
  59.3 5.9 %collective-permute-done.4 = bf16[24,9216]{1,0:T(8,128)(2,1)S(1)} collective-permute-done((bf16[24,9216]{1,0:T(8,128)(2,1)S(1)}, bf16[24,9216]{1,0:T(8,128)(2,1)S(1)}, u32[]{:S(2)}, u32[]{:S(2)}) %collective-permute-start.4) | collective-permute-done | bytes 442400 | tf_op jit(solution)/shard_map/ppermute | solution.py:87
  65.1 5.2 %collective-permute-start.5 = (bf16[24,9216]{1,0:T(8,128)(2,1)S(1)}, bf16[24,9216]{1,0:T(8,128)(2,1)S(1)}, u32[]{:S(2)}, u32[]{:S(2)}) collective-permute-start(bf16[24,9216]{1,0:T(8,128)(2,1)S(1)} %collective-permute-done.4), channel_id=1, source_target_pairs={{0,28},{4,0},{8,4},{12,8},{16,12},{20,16},{24,20},{28,24},{1,29},{... | collective-permute-start | bytes 1327112 | tf_op jit(solution)/shard_map/ppermute | solution.py:87
  70.3 0.8 constant_dynamic-update-slice_fusion.10
  71.1 7.0 %collective-permute-done.5 = bf16[24,9216]{1,0:T(8,128)(2,1)S(1)} collective-permute-done((bf16[24,9216]{1,0:T(8,128)(2,1)S(1)}, bf16[24,9216]{1,0:T(8,128)(2,1)S(1)}, u32[]{:S(2)}, u32[]{:S(2)}) %collective-permute-start.5) | collective-permute-done | bytes 442400 | tf_op jit(solution)/shard_map/ppermute | solution.py:87
  78.1 5.2 %collective-permute-start.6 = (bf16[24,9216]{1,0:T(8,128)(2,1)S(1)}, bf16[24,9216]{1,0:T(8,128)(2,1)S(1)}, u32[]{:S(2)}, u32[]{:S(2)}) collective-permute-start(bf16[24,9216]{1,0:T(8,128)(2,1)S(1)} %collective-permute-done.5), channel_id=1, source_target_pairs={{0,28},{4,0},{8,4},{12,8},{16,12},{20,16},{24,20},{28,24},{1,29},{... | collective-permute-start | bytes 1327112 | tf_op jit(solution)/shard_map/ppermute | solution.py:87
  83.3 0.8 constant_dynamic-update-slice_fusion.9
  84.1 5.0 %collective-permute-done.6 = bf16[24,9216]{1,0:T(8,128)(2,1)S(1)} collective-permute-done((bf16[24,9216]{1,0:T(8,128)(2,1)S(1)}, bf16[24,9216]{1,0:T(8,128)(2,1)S(1)}, u32[]{:S(2)}, u32[]{:S(2)}) %collective-permute-start.6) | collective-permute-done | bytes 442400 | tf_op jit(solution)/shard_map/ppermute | solution.py:87
  89.1 0.8 constant_dynamic-update-slice_fusion.8
  89.9 0.8 constant_dynamic-update-slice_fusion.7
  91.5 0.8 constant_dynamic-update-slice_fusion.5
  92.3 0.8 constant_dynamic-update-slice_fusion.4
  93.1 0.8 constant_dynamic-update-slice_fusion.3
  93.9 0.8 constant_dynamic-update-slice_fusion.2
  94.7 0.8 constant_dynamic-update-slice_fusion.1
  95.5 0.8 constant_dynamic-update-slice_fusion
  96.3 9.6 %fusion.31 = (f32[192]{0:T(256)S(1)}, f32[192,1024]{1,0:T(8,128)S(1)}) fusion(bf16[9216,1024]{1,0:T(8,128)(2,1)} %param.8, bf16[384,9216]{1,0:T(8,128)(2,1)} %constant_dynamic-update-slice_fusion, s32[]{:T(128)S(6)} %select_n.37), kind=kOutput, calls=%fused_computation.67 | convolution fusion | flops 3624075008 | bytes 23200516 | tf_op jit(solution)/shard_map/dot_general | solution.py:94
  106.0 8.6 %fusion.30 = (f32[192]{0:T(256)S(1)}, f32[192,1024]{1,0:T(8,128)S(1)}) fusion(bf16[9216,1024]{1,0:T(8,128)(2,1)} %param.7, bf16[384,9216]{1,0:T(8,128)(2,1)S(1)} %copy-done.1, s32[]{:T(128)S(6)} %select_n.37), kind=kOutput, calls=%fused_computation.66 | convolution fusion | flops 3624075008 | bytes 23200516 | tf_op jit(solution)/shard_map/dot_general | solution.py:93
  116.0 6.5 %all-to-all-start.3 = ((f32[8,1,24]{2,1,0:T(1,128)}), f32[8,1,24]{2,1,0:T(1,128)S(1)}, u32[]{:S(2)}, u32[]{:S(2)}) async-start(f32[8,1,24]{2,1,0:T(1,128)} %all_to_all.60), calls=%async_computation.3 | async-start | bytes 8192 | tf_op jit(solution)/shard_map/all_to_all | solution.py:106
  123.2 5.8 %all-to-all-done.3 = f32[8,1,24]{2,1,0:T(1,128)S(1)} async-done(((f32[8,1,24]{2,1,0:T(1,128)}), f32[8,1,24]{2,1,0:T(1,128)S(1)}, u32[]{:S(2)}, u32[]{:S(2)}) %all-to-all-start.3) | async-done | bytes 800 | tf_op jit(solution)/shard_map/all_to_all | solution.py:106
  129.0 3.3 %all-to-all-start.1 = ((f32[8,1,24]{2,1,0:T(1,128)}), f32[8,1,24]{2,1,0:T(1,128)S(1)}, u32[]{:S(2)}, u32[]{:S(2)}) async-start(f32[8,1,24]{2,1,0:T(1,128)} %all_to_all.54), calls=%async_computation.1 | async-start | bytes 8192 | tf_op jit(solution)/shard_map/all_to_all | solution.py:106
  133.0 5.8 %all-to-all-done.1 = f32[8,1,24]{2,1,0:T(1,128)S(1)} async-done(((f32[8,1,24]{2,1,0:T(1,128)}), f32[8,1,24]{2,1,0:T(1,128)S(1)}, u32[]{:S(2)}, u32[]{:S(2)}) %all-to-all-start.1) | async-done | bytes 800 | tf_op jit(solution)/shard_map/all_to_all | solution.py:106
  138.7 3.3 %all-to-all-start.4 = ((f32[8,1,24]{2,1,0:T(1,128)}), f32[8,1,24]{2,1,0:T(1,128)S(1)}, u32[]{:S(2)}, u32[]{:S(2)}) async-start(f32[8,1,24]{2,1,0:T(1,128)} %all_to_all.64), calls=%async_computation.4 | async-start | bytes 8192 | tf_op jit(solution)/shard_map/all_to_all | solution.py:106
  142.7 5.7 %all-to-all-done.4 = f32[8,1,24]{2,1,0:T(1,128)S(1)} async-done(((f32[8,1,24]{2,1,0:T(1,128)}), f32[8,1,24]{2,1,0:T(1,128)S(1)}, u32[]{:S(2)}, u32[]{:S(2)}) %all-to-all-start.4) | async-done | bytes 800 | tf_op jit(solution)/shard_map/all_to_all | solution.py:106
  148.5 3.2 %all-to-all-start = ((f32[8,1,24]{2,1,0:T(1,128)}), f32[8,1,24]{2,1,0:T(1,128)S(1)}, u32[]{:S(2)}, u32[]{:S(2)}) async-start(f32[8,1,24]{2,1,0:T(1,128)} %all_to_all.52), calls=%async_computation | async-start | bytes 8192 | tf_op jit(solution)/shard_map/all_to_all | solution.py:106
  152.4 5.7 %all-to-all-done = f32[8,1,24]{2,1,0:T(1,128)S(1)} async-done(((f32[8,1,24]{2,1,0:T(1,128)}), f32[8,1,24]{2,1,0:T(1,128)S(1)}, u32[]{:S(2)}, u32[]{:S(2)}) %all-to-all-start) | async-done | bytes 800 | tf_op jit(solution)/shard_map/all_to_all | solution.py:106
  158.1 3.3 %all-to-all-start.2 = ((f32[8,1,24]{2,1,0:T(1,128)}), f32[8,1,24]{2,1,0:T(1,128)S(1)}, u32[]{:S(2)}, u32[]{:S(2)}) async-start(f32[8,1,24]{2,1,0:T(1,128)} %all_to_all.56), calls=%async_computation.2 | async-start | bytes 8192 | tf_op jit(solution)/shard_map/all_to_all | solution.py:106
  164.1 3.8 %all-to-all-done.2 = f32[8,1,24]{2,1,0:T(1,128)S(1)} async-done(((f32[8,1,24]{2,1,0:T(1,128)}), f32[8,1,24]{2,1,0:T(1,128)S(1)}, u32[]{:S(2)}, u32[]{:S(2)}) %all-to-all-start.2) | async-done | bytes 800 | tf_op jit(solution)/shard_map/all_to_all | solution.py:106
  167.9 3.2 %all-to-all-start.5 = ((f32[8,1,24]{2,1,0:T(1,128)}), f32[8,1,24]{2,1,0:T(1,128)S(1)}, u32[]{:S(2)}, u32[]{:S(2)}) async-start(f32[8,1,24]{2,1,0:T(1,128)} %all_to_all.67), calls=%async_computation.5 | async-start | bytes 8192 | tf_op jit(solution)/shard_map/all_to_all | solution.py:106
  171.2 6.4 %all-to-all-done.5 = f32[8,1,24]{2,1,0:T(1,128)S(1)} async-done(((f32[8,1,24]{2,1,0:T(1,128)}), f32[8,1,24]{2,1,0:T(1,128)S(1)}, u32[]{:S(2)}, u32[]{:S(2)}) %all-to-all-start.5) | async-done | bytes 800 | tf_op jit(solution)/shard_map/all_to_all | solution.py:106
  177.6 3.3 %all-to-all-start.6 = ((f32[8,1,24]{2,1,0:T(1,128)}), f32[8,1,24]{2,1,0:T(1,128)S(1)}, u32[]{:S(2)}, u32[]{:S(2)}) async-start(f32[8,1,24]{2,1,0:T(1,128)} %all_to_all.69), calls=%async_computation.6 | async-start | bytes 8192 | tf_op jit(solution)/shard_map/all_to_all | solution.py:106
  182.2 5.1 %all-to-all-done.6 = f32[8,1,24]{2,1,0:T(1,128)S(1)} async-done(((f32[8,1,24]{2,1,0:T(1,128)}), f32[8,1,24]{2,1,0:T(1,128)S(1)}, u32[]{:S(2)}, u32[]{:S(2)}) %all-to-all-start.6) | async-done | bytes 800 | tf_op jit(solution)/shard_map/all_to_all | solution.py:106
  187.6 5.6 %all-reduce.8 = (f32[96]{0:T(128)S(1)}, f32[96]{0:T(128)S(1)}, f32[96]{0:T(128)S(1)}, f32[96]{0:T(128)S(1)}, f32[96]{0:T(128)S(1)}, /*index=5*/f32[96]{0:T(128)S(1)}, f32[96]{0:T(128)S(1)}) all-reduce(f32[96]{0:T(128)S(1)} %dynamic-update-slice, f32[96]{0:T(128)S(1)} %dynamic-update-slice.1, ...), channel_id=2, replica_groups=mesh['tok'=8,'vocab'=4] {'vocab'}, use_global_device_ids=true, to_apply=%add | all-reduce | flops 672 | bytes 5376
  (60 shorter events, 10.2 us)
Async XLA Ops:
  0.6 89.3 %copy-start = (bf16[24,9216]{1,0:T(8,128)(2,1)S(1)}, bf16[24,9216]{1,0:T(8,128)(2,1)}, u32[]{:S(2)}) copy-start(bf16[24,9216]{1,0:T(8,128)(2,1)} %param.6) | copy-start | bytes 1327108
  0.6 21.1 %collective-permute-start = (bf16[24,9216]{1,0:T(8,128)(2,1)}, bf16[24,9216]{1,0:T(8,128)(2,1)S(1)}, u32[]{:S(2)}, u32[]{:S(2)}) collective-permute-start(bf16[24,9216]{1,0:T(8,128)(2,1)} %param.6), channel_id=1, source_target_pairs={{0,28},{4,0},{8,4},{12,8},{16,12},{20,16},{24,20},{28,24},{1,29},{... | collective-permute-start | bytes 1327112 | tf_op jit(solution)/shard_map/ppermute | solution.py:87
  21.8 10.3 %collective-permute-start.1 = (bf16[24,9216]{1,0:T(8,128)(2,1)S(1)}, bf16[24,9216]{1,0:T(8,128)(2,1)S(1)}, u32[]{:S(2)}, u32[]{:S(2)}) collective-permute-start(bf16[24,9216]{1,0:T(8,128)(2,1)S(1)} %collective-permute-done), channel_id=1, source_target_pairs={{0,28},{4,0},{8,4},{12,8},{16,12},{20,16},{24,20},{28,24},{1,29},{... | collective-permute-start | bytes 1327112 | tf_op jit(solution)/shard_map/ppermute | solution.py:87
  32.1 10.2 %collective-permute-start.2 = (bf16[24,9216]{1,0:T(8,128)(2,1)S(1)}, bf16[24,9216]{1,0:T(8,128)(2,1)S(1)}, u32[]{:S(2)}, u32[]{:S(2)}) collective-permute-start(bf16[24,9216]{1,0:T(8,128)(2,1)S(1)} %collective-permute-done.1), channel_id=1, source_target_pairs={{0,28},{4,0},{8,4},{12,8},{16,12},{20,16},{24,20},{28,24},{1,29},{... | collective-permute-start | bytes 1327112 | tf_op jit(solution)/shard_map/ppermute | solution.py:87
  42.3 11.0 %collective-permute-start.3 = (bf16[24,9216]{1,0:T(8,128)(2,1)S(1)}, bf16[24,9216]{1,0:T(8,128)(2,1)S(1)}, u32[]{:S(2)}, u32[]{:S(2)}) collective-permute-start(bf16[24,9216]{1,0:T(8,128)(2,1)S(1)} %collective-permute-done.2), channel_id=1, source_target_pairs={{0,28},{4,0},{8,4},{12,8},{16,12},{20,16},{24,20},{28,24},{1,29},{... | collective-permute-start | bytes 1327112 | tf_op jit(solution)/shard_map/ppermute | solution.py:87
  53.3 11.8 %collective-permute-start.4 = (bf16[24,9216]{1,0:T(8,128)(2,1)S(1)}, bf16[24,9216]{1,0:T(8,128)(2,1)S(1)}, u32[]{:S(2)}, u32[]{:S(2)}) collective-permute-start(bf16[24,9216]{1,0:T(8,128)(2,1)S(1)} %collective-permute-done.3), channel_id=1, source_target_pairs={{0,28},{4,0},{8,4},{12,8},{16,12},{20,16},{24,20},{28,24},{1,29},{... | collective-permute-start | bytes 1327112 | tf_op jit(solution)/shard_map/ppermute | solution.py:87
  65.1 13.0 %collective-permute-start.5 = (bf16[24,9216]{1,0:T(8,128)(2,1)S(1)}, bf16[24,9216]{1,0:T(8,128)(2,1)S(1)}, u32[]{:S(2)}, u32[]{:S(2)}) collective-permute-start(bf16[24,9216]{1,0:T(8,128)(2,1)S(1)} %collective-permute-done.4), channel_id=1, source_target_pairs={{0,28},{4,0},{8,4},{12,8},{16,12},{20,16},{24,20},{28,24},{1,29},{... | collective-permute-start | bytes 1327112 | tf_op jit(solution)/shard_map/ppermute | solution.py:87
  78.1 11.0 %collective-permute-start.6 = (bf16[24,9216]{1,0:T(8,128)(2,1)S(1)}, bf16[24,9216]{1,0:T(8,128)(2,1)S(1)}, u32[]{:S(2)}, u32[]{:S(2)}) collective-permute-start(bf16[24,9216]{1,0:T(8,128)(2,1)S(1)} %collective-permute-done.5), channel_id=1, source_target_pairs={{0,28},{4,0},{8,4},{12,8},{16,12},{20,16},{24,20},{28,24},{1,29},{... | collective-permute-start | bytes 1327112 | tf_op jit(solution)/shard_map/ppermute | solution.py:87
  96.3 9.6 %copy-start.1 = (bf16[384,9216]{1,0:T(8,128)(2,1)S(1)}, bf16[384,9216]{1,0:T(8,128)(2,1)}, u32[]{:S(2)}) copy-start(bf16[384,9216]{1,0:T(8,128)(2,1)} %constant_dynamic-update-slice_fusion) | copy-start | bytes 21233668
  106.0 55.5 %copy-start.2 = (u32[32]{0:T(128)S(1)}, u32[32]{0:T(128)}, u32[]{:S(2)}) copy-start(u32[32]{0:T(128)} %constant.77) | copy-start | bytes 388
  116.0 13.0 %all-to-all-start.3 = ((f32[8,1,24]{2,1,0:T(1,128)}), f32[8,1,24]{2,1,0:T(1,128)S(1)}, u32[]{:S(2)}, u32[]{:S(2)}) async-start(f32[8,1,24]{2,1,0:T(1,128)} %all_to_all.60), calls=%async_computation.3 | async-start | bytes 8192 | tf_op jit(solution)/shard_map/all_to_all | solution.py:106
  129.0 9.8 %all-to-all-start.1 = ((f32[8,1,24]{2,1,0:T(1,128)}), f32[8,1,24]{2,1,0:T(1,128)S(1)}, u32[]{:S(2)}, u32[]{:S(2)}) async-start(f32[8,1,24]{2,1,0:T(1,128)} %all_to_all.54), calls=%async_computation.1 | async-start | bytes 8192 | tf_op jit(solution)/shard_map/all_to_all | solution.py:106
  138.7 9.7 %all-to-all-start.4 = ((f32[8,1,24]{2,1,0:T(1,128)}), f32[8,1,24]{2,1,0:T(1,128)S(1)}, u32[]{:S(2)}, u32[]{:S(2)}) async-start(f32[8,1,24]{2,1,0:T(1,128)} %all_to_all.64), calls=%async_computation.4 | async-start | bytes 8192 | tf_op jit(solution)/shard_map/all_to_all | solution.py:106
  148.5 9.7 %all-to-all-start = ((f32[8,1,24]{2,1,0:T(1,128)}), f32[8,1,24]{2,1,0:T(1,128)S(1)}, u32[]{:S(2)}, u32[]{:S(2)}) async-start(f32[8,1,24]{2,1,0:T(1,128)} %all_to_all.52), calls=%async_computation | async-start | bytes 8192 | tf_op jit(solution)/shard_map/all_to_all | solution.py:106
  158.1 9.8 %all-to-all-start.2 = ((f32[8,1,24]{2,1,0:T(1,128)}), f32[8,1,24]{2,1,0:T(1,128)S(1)}, u32[]{:S(2)}, u32[]{:S(2)}) async-start(f32[8,1,24]{2,1,0:T(1,128)} %all_to_all.56), calls=%async_computation.2 | async-start | bytes 8192 | tf_op jit(solution)/shard_map/all_to_all | solution.py:106
  167.9 9.7 %all-to-all-start.5 = ((f32[8,1,24]{2,1,0:T(1,128)}), f32[8,1,24]{2,1,0:T(1,128)S(1)}, u32[]{:S(2)}, u32[]{:S(2)}) async-start(f32[8,1,24]{2,1,0:T(1,128)} %all_to_all.67), calls=%async_computation.5 | async-start | bytes 8192 | tf_op jit(solution)/shard_map/all_to_all | solution.py:106
  177.6 9.7 %all-to-all-start.6 = ((f32[8,1,24]{2,1,0:T(1,128)}), f32[8,1,24]{2,1,0:T(1,128)S(1)}, u32[]{:S(2)}, u32[]{:S(2)}) async-start(f32[8,1,24]{2,1,0:T(1,128)} %all_to_all.69), calls=%async_computation.6 | async-start | bytes 8192 | tf_op jit(solution)/shard_map/all_to_all | solution.py:106
